TPU v7x, 32 devices: a whole 2x2x4 slice. The times are simulated.
32 devices in a mesh: dp: 4 (over y, x), owner: 8 (over z, core).
Axes of the slice: x: 2, y: 2, z: 4, core: 2. Of those that a mesh axis runs over, the one named last changes fastest.
Arguments:
- partial_grads: bfloat16 [4, 48, 1024, 1024], P('dp', None, 'owner'), may hold values from -2.09375 to 2.09375
- owner_map: int32 [48], replicated, may hold values from 0 to 7, as said below
- left_stats: float32 [8, 12, 1024, 1024], P('owner', None, 'dp'), may hold values from -1.8 to 1.8
- right_stats: float32 [8, 12, 1024, 1024], P('owner', None, 'dp'), may hold values from -1.8 to 1.8
- left_roots: bfloat16 [8, 12, 1024, 1024], P('owner', None, 'dp'), as said below
- right_roots: bfloat16 [8, 12, 1024, 1024], P('owner', None, 'dp'), as said below
Outputs:
- direction: bfloat16 [48, 1024, 1024], P(None, ('dp', 'owner'))
- new_left_stats: float32 [8, 12, 1024, 1024], P('owner', None, 'dp')
- new_right_stats: float32 [8, 12, 1024, 1024], P('owner', None, 'dp')
Inputs may be any that keep to these rules, and one draw needn't show every extreme that they name: `owner_map`: no owner index holds more than 12 blocks, and some owner holds exactly 12. `left_roots`: each block is dense and not symmetric; its diagonal entries are of order one and its off-diagonal entries are small. `right_roots`: each block is dense and not symmetric; its diagonal entries are of order one and its off-diagonal entries are small.
All inputs are finite; a program needn't handle non-finite values.
Results may differ from a plain program's by a relative error of at most 0.017.
Values may be sent and summed in bfloat16 or wider, within the bound.
No kernel may reach another device: no remote copies, remote signals or barrier semaphores. Data moves between devices by JAX's collectives and lax.ppermute only.
A program may use at most 256 MiB of HBM per device.

v0:
```python
import jax
import jax.numpy as jnp
from jax import lax
from jax.sharding import PartitionSpec as P

D_MODEL = 2560
D_IN = 10576
D_INNER = 5120
TILE = 1024


stat_decay = 0.999


def extents(count):
    index = jnp.arange(count, dtype=jnp.int32)
    in_cols = -(-D_IN // TILE)
    out_cols = -(-D_MODEL // TILE)
    in_count = -(-D_MODEL // TILE) * in_cols
    is_in = index < in_count
    other = jnp.maximum(index - in_count, 0)
    rows = jnp.where(
        is_in,
        jnp.minimum(TILE, D_MODEL - index // in_cols * TILE),
        jnp.minimum(TILE, D_INNER - other // out_cols * TILE),
    )
    cols = jnp.where(
        is_in,
        jnp.minimum(TILE, D_IN - index % in_cols * TILE),
        jnp.minimum(TILE, D_MODEL - other % out_cols * TILE),
    )
    return (rows, cols)


def body(partial_grads, owner_map, left_stats, right_stats, left_roots, right_roots):
    owners = lax.axis_size("owner")
    owner_here = lax.axis_index("owner")
    dp_here = lax.axis_index("dp")
    tiles = owner_map.shape[0]
    slots = left_stats.shape[1]
    lanes = left_stats.shape[2]
    tile = left_stats.shape[3]
    piece = partial_grads.shape[2]
    rows, cols = extents(tiles)
    line = jnp.arange(tile, dtype=jnp.int32)
    piece_rows = owner_here * piece + jnp.arange(piece, dtype=jnp.int32)
    source_mask = (piece_rows[None, :, None] < rows[:, None, None]) & (
        line[None, None, :] < cols[:, None, None]
    )
    local = jnp.where(source_mask, partial_grads[0], jnp.zeros((), jnp.bfloat16))
    ids = jnp.arange(tiles, dtype=jnp.int32)
    same = (owner_map[:, None] == owner_map[None, :]) & (ids[None, :] < ids[:, None])
    slot = jnp.sum(same.astype(jnp.int32), axis=1)
    picks = (slot[None, None, :] == jnp.arange(slots, dtype=jnp.int32)[:, None, None]) & (
        owner_map[None, None, :] == jnp.arange(owners, dtype=jnp.int32)[None, :, None]
    )
    tile_of = jnp.sum(jnp.where(picks, ids[None, None, :], 0), axis=2)
    filled = jnp.any(picks, axis=2)
    shares = lax.psum_scatter(
        local.astype(jnp.float32).astype(jnp.bfloat16), "dp", scatter_dimension=1, tiled=True
    )
    taken = jnp.take(shares, tile_of.reshape(-1), axis=0)
    taken = taken.reshape((slots, owners) + shares.shape[1:])
    arrived = lax.all_to_all(
        jnp.where(filled[:, :, None, None], taken, jnp.zeros((), shares.dtype)),
        "owner",
        split_axis=1,
        concat_axis=1,
        tiled=True,
    )
    grads = lax.all_gather(arrived, "dp", axis=2, tiled=True).reshape(slots, tile, tile)
    grad_rows = lax.dynamic_slice_in_dim(grads, dp_here * lanes, lanes, 1)
    grad_cols = lax.dynamic_slice_in_dim(grads, dp_here * lanes, lanes, 2)
    left_gram = jnp.einsum("srk,stk->srt", grad_rows, grads, preferred_element_type=jnp.float32)
    right_gram = jnp.einsum("skc,skt->sct", grad_cols, grads, preferred_element_type=jnp.float32)
    new_left = stat_decay * left_stats[0] + (1.0 - stat_decay) * left_gram
    new_right = stat_decay * right_stats[0] + (1.0 - stat_decay) * right_gram
    left_part = jnp.einsum(
        "srk,skc->src", left_roots[0], grads, preferred_element_type=jnp.float32
    ).astype(jnp.bfloat16)
    product = jnp.einsum(
        "srk,skc->src",
        left_part,
        lax.all_gather(right_roots[0], "dp", axis=1, tiled=True),
        preferred_element_type=jnp.float32,
    )
    tile_here = lax.dynamic_index_in_dim(tile_of, owner_here, 1, keepdims=False)
    rows_here = jnp.take(rows, tile_here)
    cols_here = jnp.take(cols, tile_here)
    block_rows = dp_here * lanes + jnp.arange(lanes, dtype=jnp.int32)
    out_mask = (block_rows[None, :, None] < rows_here[:, None, None]) & (
        line[None, None, :] < cols_here[:, None, None]
    )
    result = jnp.where(out_mask, product, jnp.float32(0.0)).astype(jnp.bfloat16)
    sub_rows = lanes // owners
    returned = lax.all_to_all(
        result.reshape(slots, owners, sub_rows, tile),
        "owner",
        split_axis=1,
        concat_axis=1,
        tiled=True,
    )
    flat = returned.reshape(slots * owners, sub_rows, tile)
    direction = jnp.take(flat, slot * owners + owner_map, axis=0)
    return (direction, new_left[None], new_right[None])


def solution(mesh):
    placed = (
        P("dp", None, "owner", None),
        P(),
        P("owner", None, "dp", None),
        P("owner", None, "dp", None),
        P("owner", None, "dp", None),
        P("owner", None, "dp", None),
    )
    return jax.shard_map(
        body,
        mesh=mesh,
        in_specs=placed,
        out_specs=(
            P(None, ("dp", "owner"), None),
            P("owner", None, "dp", None),
            P("owner", None, "dp", None),
        ),
        check_vma=False,
    )
```

profile of v0, /device:TPU:0, one launch (start us, length us, event | category | flops | bytes accessed | tf_op | source)
XLA Modules:
  0.0 949.2 jit_solution(2275614357485524921)
XLA Ops:
  7.2 0.0 reduce-scatter.2.cloned.1.call-start
  7.2 0.1 iota_compare_fusion
  7.4 0.1 broadcast_compare_fusion
  7.4 12.1 %and_select_fusion = bf16[48,128,1024]{2,1,0:T(8,128)(2,1)} fusion(bf16[1,48,128,1024]{3,2,1,0:T(8,128)(2,1)} %param.8, pred[48,1024]{1,0:T(8,128)(4,1)S(1)} %iota_compare_fusion, pred[48,128]{1,0:T(8,128)(4,1)S(1)} %broadcast_compare_fusion), kind=kLoop, calls=%fused_computation.6 | loop fusion | flops 12582912 | bytes 25221120 | tf_op jit(solution)/shard_map/jit(_where)/select_n | solution.py:50
  19.5 0.0 copy-start
  19.5 0.0 reduce-scatter.2.cloned.1.call-update
  19.5 0.0 all-gather.4.cloned.1.call-start
  19.6 0.6 copy-done
  20.2 0.2 convert_reduce_fusion
  20.4 0.3 fusion.25
  20.7 0.1 reshape.284
  20.8 0.3 and_reduce_fusion
  21.1 121.9 %reduce-scatter.2.cloned.1.call-done = bf16[48,32,1024]{2,1,0:T(8,128)(2,1)} async-done(((bf16[48,128,1024]{2,1,0:T(8,128)(2,1)}), bf16[48,32,1024]{2,1,0:T(8,128)(2,1)}) %reduce-scatter.2.cloned.1.call-update) | async-done | bytes 3145744 | tf_op jit(solution)/shard_map/reduce_scatter | solution.py:59
  143.0 7.9 gather_fusion
  150.9 4.0 select_select_fusion
  154.9 1.3 copy.27
  156.2 143.4 %all_to_all.10 = bf16[12,8,32,1024]{3,2,0,1:T(8,128)(2,1)} all-to-all(bf16[12,8,32,1024]{3,2,0,1:T(8,128)(2,1)S(1)} %copy.27), channel_id=1, replica_groups=mesh['dp'=4,'owner'=8] {'owner'}, dimensions={1} | all-to-all | bytes 12582912 | tf_op jit(solution)/shard_map/all_to_all | solution.py:64
  299.7 0.0 all-gather.4.cloned.1.call-update
  299.7 0.0 all-gather.6.cloned.1.call-start
  299.7 0.7 all-gather.6.cloned.1.call-update
  300.4 0.2 dynamic-slice_reduce_fusion
  300.6 0.7 gather_fusion.3
  301.3 0.7 gather_fusion.2
  302.0 0.1 broadcast_compare_fusion.1
  302.1 0.1 iota_compare_fusion.1
  302.1 223.2 %all-gather.4.cloned.1.call-done = bf16[12,8,128,1024]{3,2,0,1:T(8,128)(2,1)} async-done(((bf16[12,8,32,1024]{3,2,0,1:T(8,128)(2,1)}), bf16[12,8,128,1024]{3,2,0,1:T(8,128)(2,1)}) %all-gather.4.cloned.1.call-update) | async-done | bytes 25165840 | tf_op jit(solution)/shard_map/all_gather | solution.py:71
  525.4 34.1 %copy.28 = bf16[12,8,128,1024]{2,1,3,0:T(8,128)(2,1)} copy(bf16[12,8,128,1024]{3,2,0,1:T(8,128)(2,1)} %all-gather.4.cloned.1.call-done) | data formatting | bytes 50331648 | tf_op jit(solution)/shard_map/all_gather | solution.py:71
  559.5 37.4 %reshape.285 = bf16[12,1024,1024]{1,2,0:T(8,128)(2,1)} reshape(bf16[12,8,128,1024]{2,1,3,0:T(8,128)(2,1)} %copy.28) | data formatting | bytes 50331648 | tf_op jit(solution)/shard_map/reshape | solution.py:71
  596.9 158.0 %all-gather.6.cloned.1.call-done = bf16[1,12,1024,1024]{3,2,1,0:T(8,128)(2,1)} async-done(((bf16[1,12,256,1024]{3,2,1,0:T(8,128)(2,1)}), bf16[1,12,1024,1024]{3,2,1,0:T(8,128)(2,1)}) %all-gather.6.cloned.1.call-update) | async-done | bytes 25165840 | tf_op jit(solution)/shard_map/all_gather | solution.py:84
  754.9 25.0 %select_convert_fusion = bf16[12,256,1024]{2,1,0:T(8,128)(2,1)} fusion(pred[12,1024]{1,0:T(8,128)(4,1)S(1)} %iota_compare_fusion.1, pred[12,256]{1,0:T(8,128)(4,1)S(1)} %broadcast_compare_fusion.1, bf16[1,12,1024,1024]{3,2,1,0:T(8,128)(2,1)} %all-gather.6.cloned.1.call-done, bf16[12,1024,1024]{1,2,0:T(8,128)(2,1)} %reshape.285, ...), kind=kOutput, calls=%fused_computation.11 | convolution fusion | flops 12897484800 | bytes 62929920 | tf_op jit(solution)/shard_map/srk,skc->src/dot_general | solution.py:81
  779.8 6.8 copy.30
  786.6 4.9 all-to-all-start.1
  791.6 20.5 %fusion.3 = f32[1,12,256,1024]{3,2,1,0:T(8,128)} fusion(f32[1,12,256,1024]{3,2,1,0:T(8,128)} %param.10, bf16[12,1024,1024]{1,2,0:T(8,128)(2,1)} %reshape.285, s32[]{:T(128)S(6)} %select_n.138), kind=kOutput, calls=%fused_computation.10 | convolution fusion | flops 6451888128 | bytes 56623108 | tf_op jit(solution)/shard_map/srk,stk->srt/dot_general | solution.py:74
  812.1 20.2 %fusion.2 = f32[1,12,256,1024]{3,2,1,0:T(8,128)} fusion(f32[1,12,256,1024]{3,2,1,0:T(8,128)} %param.11, bf16[12,1024,1024]{1,2,0:T(8,128)(2,1)} %reshape.285, s32[]{:T(128)S(6)} %select_n.138), kind=kOutput, calls=%fused_computation.8 | convolution fusion | flops 6451888128 | bytes 56623108 | tf_op jit(solution)/shard_map/skc,skt->sct/dot_general | solution.py:75
  832.2 98.1 %all-to-all-done.1 = bf16[12,8,32,1024]{3,2,0,1:T(8,128)(2,1)} async-done(((bf16[12,8,32,1024]{3,2,0,1:T(8,128)(2,1)}), bf16[12,8,32,1024]{3,2,0,1:T(8,128)(2,1)}, u32[]{:S(2)}, u32[]{:S(2)}) %all-to-all-start.1) | async-done | bytes 6291488 | tf_op jit(solution)/shard_map/all_to_all | solution.py:96
  930.3 6.8 copy.31
  937.1 3.5 gather_fusion.1
  940.6 2.0 broadcast_select_fusion
  (13 shorter events, 0.1 us)
Async XLA Ops:
  7.2 135.8 %reduce-scatter.2.cloned.1.call-start = ((), (), s32[]{:S(2)}) async-start(), calls=%async_computation.3 | async-start | bytes 15728640 | tf_op jit(solution)/shard_map/reduce_scatter | solution.py:59
  19.5 0.7 copy-start
  19.5 505.8 %all-gather.4.cloned.1.call-start = ((), (), s32[]{:S(2)}) async-start(), calls=%async_computation.4 | async-start | bytes 31457280 | tf_op jit(solution)/shard_map/all_gather | solution.py:71
  299.7 455.2 %all-gather.6.cloned.1.call-start = ((), (), s32[]{:S(2)}) async-start(), calls=%async_computation.5 | async-start | bytes 31457280 | tf_op jit(solution)/shard_map/all_gather | solution.py:84
  786.6 143.7 %all-to-all-start.1 = ((bf16[12,8,32,1024]{3,2,0,1:T(8,128)(2,1)}), bf16[12,8,32,1024]{3,2,0,1:T(8,128)(2,1)}, u32[]{:S(2)}, u32[]{:S(2)}) async-start(bf16[12,8,32,1024]{3,2,0,1:T(8,128)(2,1)} %copy.30), calls=%async_computation.2 | async-start | bytes 12582912 | tf_op jit(solution)/shard_map/all_to_all | solution.py:96
Sparse Core Ops, SparseCore 0:
  19.7 123.2 reduce-scatter.1
  299.8 225.5 all-gather.3
  527.2 227.5 all-gather.5
where the time goes:
time: 951 us; the launch traced here: 949 us
  waiting for transfers between devices  602 us (63%)
  blocking collectives  143 us (15%)
  local copies, waits for them, and re-layouts  100 us (11%)
  matrix products  65.6 us (7%)
  other arithmetic  19.2 us (2%)
  between operations  13.9 us (1%)
    all_gather x1, waiting for transfers between devices, body(): lax.all_gather(arrived, 'dp', axis=2, tiled=True).reshape(slots, tile, tile)  223 us
    all_gather x1, waiting for transfers between devices, body(): lax.all_gather(right_roots[0], 'dp', axis=1, tiled=True)  158 us
    all_to_all x1, blocking collectives, body(): lax.all_to_all(jnp.where(filled[:, :, None, None], taken, jnp.zeros((), s...  143 us
    reduce_scatter x1, waiting for transfers between devices, body(): lax.psum_scatter(local.astype(jnp.float32).astype(jnp.bfloat16), 'dp', sc...  122 us
    all_to_all x1, waiting for transfers between devices, body(): lax.all_to_all(result.reshape(slots, owners, sub_rows, tile), 'owner', sp...  98.1 us
    reshape x1, local copies, waits for them, and re-layouts, body(): lax.all_gather(arrived, 'dp', axis=2, tiled=True).reshape(slots, tile, tile)  37.4 us
    all_gather x1, local copies, waits for them, and re-layouts, body(): lax.all_gather(arrived, 'dp', axis=2, tiled=True).reshape(slots, tile, tile)  34.1 us
    dot_general x1, matrix products, body(): jnp.einsum('srk,skc->src', left_part, lax.all_gather(right_roots[0], 'dp'...  25 us
  transfers between devices with their start and end apart: 4, of which 4 were waited for; matrix products, arithmetic and copies ran while one was open for 12% of the time, Pallas kernels for 0%

commit v1 on v0

v1 whole, which is shorter than its diff:
```python
import jax
import jax.numpy as jnp
from jax import lax
from jax.experimental import pallas as pl
from jax.experimental.pallas import tpu as pltpu
from jax.sharding import PartitionSpec as P


D_MODEL = 2560
D_IN = 10576
D_INNER = 5120
TILE = 1024
CHUNKS = 3


stat_decay = 0.999


def extents(count):
    index = jnp.arange(count, dtype=jnp.int32)
    in_cols = -(-D_IN // TILE)
    out_cols = -(-D_MODEL // TILE)
    in_count = -(-D_MODEL // TILE) * in_cols
    is_in = index < in_count
    other = jnp.maximum(index - in_count, 0)
    rows = jnp.where(
        is_in,
        jnp.minimum(TILE, D_MODEL - index // in_cols * TILE),
        jnp.minimum(TILE, D_INNER - other // out_cols * TILE),
    )
    cols = jnp.where(
        is_in,
        jnp.minimum(TILE, D_IN - index % in_cols * TILE),
        jnp.minimum(TILE, D_MODEL - other % out_cols * TILE),
    )
    return (rows, cols)


def bounds(slots):
    chunks = min(CHUNKS, slots)
    edges = [slots * i // chunks for i in range(chunks + 1)]
    return list(zip(edges[:-1], edges[1:]))


def step_kernel(meta, g_ref, r_ref, l_ref, ls_ref, rs_ref, *rest):
    res_ref, nl_ref, nr_ref, grad = rest[-4:]
    step = pl.program_id(0)
    groups, sources, _, q, tile = g_ref.shape
    lanes = l_ref.shape[1]
    for o in range(sources):
        for d in range(groups):
            grad[pl.ds((o * groups + d) * q, q), :] = g_ref[d, o, 0]
    base = pl.multiple_of(meta[0] * lanes, lanes)
    whole = grad[...]
    left = lax.dot_general(
        l_ref[0], whole, (((1,), (0,)), ((), ())), preferred_element_type=jnp.float32
    ).astype(jnp.bfloat16)
    product = lax.dot_general(
        left,
        r_ref[:, 0].reshape(tile, tile),
        (((1,), (0,)), ((), ())),
        preferred_element_type=jnp.float32,
    )
    row = base + lax.broadcasted_iota(jnp.int32, product.shape, 0)
    col = lax.broadcasted_iota(jnp.int32, product.shape, 1)
    keep = (row < meta[1 + 2 * step]) & (col < meta[2 + 2 * step])
    result = jnp.where(keep, product, 0.0).astype(jnp.bfloat16)
    res_ref[:, 0] = result.reshape(res_ref.shape[0], res_ref.shape[2], tile)
    gram = lax.dot_general(
        grad[pl.ds(base, lanes), :], whole, (((1,), (1,)), ((), ())), preferred_element_type=jnp.float32
    )
    nl_ref[0] = stat_decay * ls_ref[0] + (1.0 - stat_decay) * gram
    gram = lax.dot_general(
        grad[:, pl.ds(base, lanes)], whole, (((0,), (0,)), ((), ())), preferred_element_type=jnp.float32
    )
    nr_ref[0] = stat_decay * rs_ref[0] + (1.0 - stat_decay) * gram


def step_call(meta, grads, rights, lefts, left_stats, right_stats, prior, first, owners):
    groups, sources, count, q, tile = grads.shape
    _, lanes = lefts.shape[:2]
    sub = lanes // owners
    parts = owners if sub % 16 == 0 else 1
    slab = pl.BlockSpec((1, lanes, tile), lambda s, m: (first + s, 0, 0))
    specs = [
        pl.BlockSpec((groups, sources, 1, q, tile), lambda s, m: (0, 0, s, 0, 0)),
        pl.BlockSpec((rights.shape[0], 1, lanes, tile), lambda s, m: (0, first + s, 0, 0)),
        slab,
        slab,
        slab,
    ]
    operands = [grads, rights, lefts, left_stats, right_stats]
    aliases = {}
    if prior is not None:
        specs += [pl.BlockSpec(memory_space=pl.ANY)] * 2
        operands += list(prior)
        aliases = {6: 1, 7: 2}
    result, new_left, new_right = pl.pallas_call(
        step_kernel,
        grid_spec=pltpu.PrefetchScalarGridSpec(
            num_scalar_prefetch=1,
            grid=(count,),
            in_specs=specs,
            out_specs=[
                pl.BlockSpec((parts, 1, lanes // parts, tile), lambda s, m: (0, s, 0, 0)),
                slab,
                slab,
            ],
            scratch_shapes=[pltpu.VMEM((tile, tile), jnp.bfloat16)],
        ),
        out_shape=[
            jax.ShapeDtypeStruct((parts, count, lanes // parts, tile), jnp.bfloat16),
            jax.ShapeDtypeStruct(left_stats.shape, jnp.float32),
            jax.ShapeDtypeStruct(right_stats.shape, jnp.float32),
        ],
        input_output_aliases=aliases,
        cost_estimate=pl.CostEstimate(
            flops=8 * count * lanes * tile * tile,
            bytes_accessed=count * (4 * tile * tile + 20 * lanes * tile),
            transcendentals=0,
        ),
        compiler_params=pltpu.CompilerParams(vmem_limit_bytes=48 * 1024 * 1024),
    )(meta, *operands)
    if parts == 1:
        result = result[0].reshape(count, owners, sub, tile).transpose(1, 0, 2, 3)
    return result, new_left, new_right


def body(partial_grads, owner_map, left_stats, right_stats, left_roots, right_roots):
    owners = lax.axis_size("owner")
    owner_here = lax.axis_index("owner")
    dp_here = lax.axis_index("dp").astype(jnp.int32)
    tiles = owner_map.shape[0]
    slots = left_stats.shape[1]
    tile = left_stats.shape[3]
    piece = partial_grads.shape[2]
    rows, cols = extents(tiles)
    line = jnp.arange(tile, dtype=jnp.int32)
    ids = jnp.arange(tiles, dtype=jnp.int32)
    shares = lax.psum_scatter(partial_grads[0], "dp", scatter_dimension=1, tiled=True)
    q = shares.shape[1]
    same = (owner_map[:, None] == owner_map[None, :]) & (ids[None, :] < ids[:, None])
    slot = jnp.sum(same.astype(jnp.int32), axis=1)
    picks = (slot[None, None, :] == jnp.arange(slots, dtype=jnp.int32)[None, :, None]) & (
        owner_map[None, None, :] == jnp.arange(owners, dtype=jnp.int32)[:, None, None]
    )
    tile_of = jnp.sum(jnp.where(picks, ids, 0), axis=2)
    rows_of = jnp.sum(jnp.where(picks, rows, 0), axis=2)
    cols_of = jnp.sum(jnp.where(picks, cols, 0), axis=2)
    rows_here = lax.dynamic_index_in_dim(rows_of, owner_here, 0, keepdims=False)
    cols_here = lax.dynamic_index_in_dim(cols_of, owner_here, 0, keepdims=False)
    extent_here = jnp.stack([rows_here, cols_here], axis=1)
    share_rows = owner_here * piece + dp_here * q + jnp.arange(q, dtype=jnp.int32)
    shares, roots = lax.optimization_barrier((shares, right_roots[0]))
    rights = lax.all_gather(roots, "dp", axis=0)
    prior = None
    direction = None

    def place(direction, returned, number):
        first, last = bounds(slots)[number]
        count = last - first
        flat = returned.reshape((owners * count,) + returned.shape[2:])
        local = slot - first
        here = (local >= 0) & (local < count)
        spot = owner_map * count + jnp.clip(local, 0, count - 1)
        chosen = flat.at[spot].get(mode="promise_in_bounds")
        if direction is None:
            return chosen
        return jnp.where(here[:, None, None], chosen, direction)

    for number, (first, last) in enumerate(bounds(slots)):
        count = last - first
        taken = shares.at[tile_of[:, first:last].reshape(-1)].get(mode="promise_in_bounds")
        taken = taken.reshape((owners, count) + shares.shape[1:])
        inside = (share_rows[None, None, :, None] < rows_of[:, first:last, None, None]) & (
            line[None, None, None, :] < cols_of[:, first:last, None, None]
        )
        taken = jnp.where(inside, taken, jnp.zeros((), shares.dtype))
        arrived = lax.all_to_all(taken, "owner", split_axis=0, concat_axis=0, tiled=True)
        grads = lax.all_gather(arrived, "dp", axis=0)
        if q % 16:
            grads = grads.transpose(2, 1, 0, 3, 4).reshape(1, 1, count, tile, tile)
        if number:
            grads, returned = lax.optimization_barrier((grads, returned))
            direction = place(direction, returned, number - 1)
        meta = jnp.concatenate([dp_here[None], extent_here[first:last].reshape(-1)])
        result, *prior = step_call(
            meta, grads, rights, left_roots[0], left_stats[0], right_stats[0], prior, first, owners
        )
        returned = lax.all_to_all(result, "owner", split_axis=0, concat_axis=0, tiled=True)
    direction = place(direction, returned, number)
    new_left, new_right = prior
    return (direction, new_left[None], new_right[None])


def solution(mesh):
    placed = (
        P("dp", None, "owner", None),
        P(),
        P("owner", None, "dp", None),
        P("owner", None, "dp", None),
        P("owner", None, "dp", None),
        P("owner", None, "dp", None),
    )
    return jax.shard_map(
        body,
        mesh=mesh,
        in_specs=placed,
        out_specs=(
            P(None, ("dp", "owner"), None),
            P("owner", None, "dp", None),
            P("owner", None, "dp", None),
        ),
        check_vma=False,
    )
```

time: 951 us -> 772 us (0.81)
  waiting for transfers between devices: 602 us -> 499 us
  local copies, waits for them, and re-layouts: 100 us -> 20.1 us
  matrix products: 65.6 us -> 0 us
  Pallas kernels: 0 us -> 53.9 us
  blocking collectives: 143 us -> 158 us
    dot_general x3 -> x0, matrix products: 65.6 us -> none  [the longest x1 25 us: body(): jnp.einsum('srk,skc->src', left_part, lax.all_gather(right_roots[0], 'dp'...]
    all_to_all x1 -> x3, waiting for transfers between devices: 98.1 us -> 42.5 us  [body(): lax.all_to_all(result, 'owner', split_axis=0, concat_axis=0, tiled=True)]
    pallas_call x0 -> x3, Pallas kernels: none -> 53.9 us  [step_call(): pl.pallas_call(step_kernel, grid_spec=pltpu.PrefetchScalarGridSpec(num_sc...]
    all_gather x2 -> x4, waiting for transfers between devices: 381 us -> 330 us  [the longest x1 199 us: body(): rights = lax.all_gather(roots, 'dp', axis=0)]
    reshape x3 -> x6, local copies, waits for them, and re-layouts: 44.2 us -> 0.5 us  [the longest x3 0.26 us: body(): meta = jnp.concatenate([dp_here[None], extent_here[first:last].reshape(-1)])]
    all_gather x1 -> x0, local copies, waits for them, and re-layouts: 34.1 us -> none  [body(): lax.all_gather(arrived, 'dp', axis=2, tiled=True).reshape(slots, tile, tile)]
    all_to_all x1 -> x3, blocking collectives: 143 us -> 158 us  [body(): lax.all_to_all(taken, 'owner', split_axis=0, concat_axis=0, tiled=True)]
  transfers between devices with their start and end apart: 4 -> 8, of which waited for: 4 -> 5; matrix products, arithmetic and copies ran while one was open for 12% -> 2% of each run, Pallas kernels for 0% -> 5%
where the time goes in v1:
time: 772 us
  waiting for transfers between devices  499 us (65%)
  blocking collectives  158 us (20%)
  Pallas kernels  53.9 us (7%)
  local copies, waits for them, and re-layouts  20.1 us (3%)
  starting transfers between devices  14.1 us (2%)
  between operations  13.9 us (2%)
  other arithmetic  12.6 us (2%)
    all_gather x1, waiting for transfers between devices, body(): rights = lax.all_gather(roots, 'dp', axis=0)  199 us
    all_to_all x3, blocking collectives, body(): lax.all_to_all(taken, 'owner', split_axis=0, concat_axis=0, tiled=True)  158 us
    all_gather x3, waiting for transfers between devices, body(): grads = lax.all_gather(arrived, 'dp', axis=0)  132 us
    reduce_scatter x1, waiting for transfers between devices, body(): lax.psum_scatter(partial_grads[0], 'dp', scatter_dimension=1, tiled=True)  125 us
    pallas_call x3, Pallas kernels, step_call(): pl.pallas_call(step_kernel, grid_spec=pltpu.PrefetchScalarGridSpec(num_sc...  53.9 us
    all_to_all x3, waiting for transfers between devices, body(): lax.all_to_all(result, 'owner', split_axis=0, concat_axis=0, tiled=True)  42.5 us
  transfers between devices with their start and end apart: 8, of which 5 were waited for; matrix products, arithmetic and copies ran while one was open for 2% of the time, Pallas kernels for 5%

profile of v1, /device:TPU:0, one launch (start us, length us, event | category | flops | bytes accessed | tf_op | source)
XLA Modules:
  0.0 771.6 jit_solution(10298445611721525372)
XLA Ops:
  7.2 0.7 reduce-scatter.2.cloned.1.call-update
  8.0 0.2 convert_reduce_fusion
  8.2 0.7 fusion.2
  8.9 0.1 copy.35
  9.2 0.1 copy.45
  9.2 0.1 reshape.239
  9.3 0.1 copy.44
  9.4 0.1 broadcast_compare_fusion
  9.5 0.1 iota_compare_fusion
  9.6 124.8 %reduce-scatter.2.cloned.1.call-done = bf16[48,32,1024]{2,1,0:T(8,128)(2,1)} async-done(((bf16[48,128,1024]{2,1,0:T(8,128)(2,1)}), bf16[48,32,1024]{2,1,0:T(8,128)(2,1)}) %reduce-scatter.2.cloned.1.call-update) | async-done | bytes 3145744 | tf_op jit(solution)/shard_map/reduce_scatter | solution.py:140
  134.4 2.6 gather_fusion.2
  137.0 0.8 and_select_fusion
  137.8 53.6 %all_to_all.30 = bf16[8,4,32,1024]{3,2,1,0:T(8,128)(2,1)} all-to-all(bf16[8,4,32,1024]{3,2,1,0:T(8,128)(2,1)S(1)} %and_select_fusion), channel_id=1, replica_groups=mesh['dp'=4,'owner'=8] {'owner'}, dimensions={0} | all-to-all | bytes 4194304 | tf_op jit(solution)/shard_map/all_to_all | solution.py:179
  191.5 0.7 all-gather.15.cloned.1.call-update
  192.2 0.1 copy.41
  192.3 0.1 reshape.236
  192.5 0.1 iota_compare_fusion.1
  192.6 0.7 copy-done
  193.3 2.0 gather_fusion.1
  195.3 2.7 and_select_fusion.1
  198.0 52.2 %all_to_all.31 = bf16[8,4,32,1024]{3,2,1,0:T(8,128)(2,1)} all-to-all(bf16[8,4,32,1024]{3,2,1,0:T(8,128)(2,1)S(1)} %and_select_fusion.1), channel_id=1, replica_groups=mesh['dp'=4,'owner'=8] {'owner'}, dimensions={0} | all-to-all | bytes 4194304 | tf_op jit(solution)/shard_map/all_to_all | solution.py:179
  250.3 0.1 copy.37
  250.6 0.1 iota_compare_fusion.2
  250.7 2.0 gather_fusion
  252.7 2.4 and_select_fusion.2
  255.0 52.2 %all_to_all.32 = bf16[8,4,32,1024]{3,2,1,0:T(8,128)(2,1)} all-to-all(bf16[8,4,32,1024]{3,2,1,0:T(8,128)(2,1)S(1)} %and_select_fusion.2), channel_id=1, replica_groups=mesh['dp'=4,'owner'=8] {'owner'}, dimensions={0} | all-to-all | bytes 4194304 | tf_op jit(solution)/shard_map/all_to_all | solution.py:179
  307.3 0.2 dynamic-slice_reduce_fusion.1
  307.4 0.2 dynamic-slice_reduce_fusion
  307.7 0.1 copy.42
  307.8 0.1 reshape.238
  308.0 198.5 %all-gather.15.cloned.1.call-done = bf16[48,256,1024]{2,1,0:T(8,128)(2,1)} async-done(((bf16[12,256,1024]{2,1,0:T(8,128)(2,1)}), bf16[48,256,1024]{2,1,0:T(8,128)(2,1)}) %all-gather.15.cloned.1.call-update) | async-done | bytes 25165840 | tf_op jit(solution)/shard_map/all_gather | solution.py:155
  506.5 18.4 %shard_map.85 = (bf16[8,4,32,1024]{3,2,1,0:T(8,128)(2,1)}, f32[12,256,1024]{2,1,0:T(8,128)}, f32[12,256,1024]{2,1,0:T(8,128)}) custom-call(s32[9]{0:T(128)S(1)} %pad_add_fusion.3.meta, bf16[4,8,4,32,1024]{4,3,2,1,0:T(8,128)(2,1)} %bitcast.42, bf16[4,12,256,1024]{3,2,1,0:T(8,128)(2,1)} %bitcast.26, bf16[12,256,1024]{2,1,0:T(8,128)(2,1)} %bitcast.35, ...), custom_call_target="tpu_custom_call" | custom-call | flops 8589934592 | bytes 37748736 | tf_op jit(solution)/shard_map/pallas_call | solution.py:98
  524.9 4.6 all-to-all-start.3
  529.5 0.1 copy.38
  529.6 0.1 reshape.235
  529.8 65.9 %all-gather.11.cloned.1.call-done = bf16[32,4,32,1024]{3,2,1,0:T(8,128)(2,1)} async-done(((bf16[8,4,32,1024]{3,2,1,0:T(8,128)(2,1)}), bf16[32,4,32,1024]{3,2,1,0:T(8,128)(2,1)}) %all-gather.11.cloned.1.call-update) | async-done | bytes 8388624 | tf_op jit(solution)/shard_map/all_gather | solution.py:180
  595.7 18.4 %shard_map.86 = (bf16[8,4,32,1024]{3,2,1,0:T(8,128)(2,1)}, f32[12,256,1024]{2,1,0:T(8,128)}, f32[12,256,1024]{2,1,0:T(8,128)}) custom-call(s32[9]{0:T(128)S(1)} %pad_add_fusion.2.meta, bf16[4,8,4,32,1024]{4,3,2,1,0:T(8,128)(2,1)} %bitcast.43, bf16[4,12,256,1024]{3,2,1,0:T(8,128)(2,1)} %bitcast.27, ...), custom_call_target="tpu_custom_call", output_to_operand_aliasing={{1}: (6, {}), {2}: (7, {})} | custom-call | flops 8589934592 | bytes 37748736 | tf_op jit(solution)/shard_map/pallas_call | solution.py:98
  614.1 4.7 all-to-all-start.4
  618.7 0.1 copy.34
  618.8 0.1 reshape.232
  619.0 65.9 %all-gather.9.cloned.1.call-done = bf16[32,4,32,1024]{3,2,1,0:T(8,128)(2,1)} async-done(((bf16[8,4,32,1024]{3,2,1,0:T(8,128)(2,1)}), bf16[32,4,32,1024]{3,2,1,0:T(8,128)(2,1)}) %all-gather.9.cloned.1.call-update) | async-done | bytes 8388624 | tf_op jit(solution)/shard_map/all_gather | solution.py:180
  684.9 17.2 %shard_map.87 = (bf16[8,4,32,1024]{3,2,1,0:T(8,128)(2,1)}, f32[12,256,1024]{2,1,0:T(8,128)}, f32[12,256,1024]{2,1,0:T(8,128)}) custom-call(s32[9]{0:T(128)S(1)} %pad_add_fusion.1.meta, bf16[4,8,4,32,1024]{4,3,2,1,0:T(8,128)(2,1)} %bitcast.44, bf16[4,12,256,1024]{3,2,1,0:T(8,128)(2,1)} %bitcast.28, ...), custom_call_target="tpu_custom_call", output_to_operand_aliasing={{1}: (6, {}), {2}: (7, {})} | custom-call | flops 8589934592 | bytes 37748736 | tf_op jit(solution)/shard_map/pallas_call | solution.py:98
  702.1 4.6 all-to-all-start.5
  706.7 2.5 gather_fusion.5
  709.2 4.1 gather_fusion.4
  713.3 42.5 %all-to-all-done.5 = bf16[8,4,32,1024]{3,2,1,0:T(8,128)(2,1)} async-done(((bf16[8,4,32,1024]{3,2,1,0:T(8,128)(2,1)}), bf16[8,4,32,1024]{3,2,1,0:T(8,128)(2,1)}, u32[]{:S(2)}, u32[]{:S(2)}) %all-to-all-start.5) | async-done | bytes 2097184 | tf_op jit(solution)/shard_map/all_to_all | solution.py:190
  755.8 4.3 gather_fusion.3
  760.1 5.0 select_select_fusion
  (44 shorter events, 1.1 us)
Async XLA Ops:
  7.2 127.2 %reduce-scatter.2.cloned.1.call-start = ((), (), s32[]{:S(2)}) async-start(), calls=%async_computation.7 | async-start | bytes 15728640 | tf_op jit(solution)/shard_map/reduce_scatter | solution.py:140
  7.2 0.8 copy-start.2
  7.9 300.1 %all-gather.13.cloned.1.call-start = ((), (), s32[]{:S(2)}) async-start(), calls=%async_computation.10 | async-start | bytes 10485760 | tf_op jit(solution)/shard_map/all_gather | solution.py:180
  191.4 1.9 copy-start
  191.4 315.1 %all-gather.15.cloned.1.call-start = ((), (), s32[]{:S(2)}) async-start(), calls=%async_computation.11 | async-start | bytes 31457280 | tf_op jit(solution)/shard_map/all_gather | solution.py:155
  192.1 403.5 %all-gather.11.cloned.1.call-start = ((), (), s32[]{:S(2)}) async-start(), calls=%async_computation.9 | async-start | bytes 10485760 | tf_op jit(solution)/shard_map/all_gather | solution.py:180
  250.2 434.6 %all-gather.9.cloned.1.call-start = ((), (), s32[]{:S(2)}) async-start(), calls=%async_computation.8 | async-start | bytes 10485760 | tf_op jit(solution)/shard_map/all_gather | solution.py:180
  524.9 70.8 %all-to-all-start.3 = ((bf16[8,4,32,1024]{3,2,1,0:T(8,128)(2,1)}), bf16[8,4,32,1024]{3,2,1,0:T(8,128)(2,1)S(1)}, u32[]{:S(2)}, u32[]{:S(2)}) async-start(bf16[8,4,32,1024]{3,2,1,0:T(8,128)(2,1)} %get-tuple-element.20), calls=%async_computation.4 | async-start | bytes 4194304 | tf_op jit(solution)/shard_map/all_to_all | solution.py:190
  614.1 70.8 %all-to-all-start.4 = ((bf16[8,4,32,1024]{3,2,1,0:T(8,128)(2,1)}), bf16[8,4,32,1024]{3,2,1,0:T(8,128)(2,1)}, u32[]{:S(2)}, u32[]{:S(2)}) async-start(bf16[8,4,32,1024]{3,2,1,0:T(8,128)(2,1)} %get-tuple-element.24), calls=%async_computation.5 | async-start | bytes 4194304 | tf_op jit(solution)/shard_map/all_to_all | solution.py:190
  702.1 53.7 %all-to-all-start.5 = ((bf16[8,4,32,1024]{3,2,1,0:T(8,128)(2,1)}), bf16[8,4,32,1024]{3,2,1,0:T(8,128)(2,1)}, u32[]{:S(2)}, u32[]{:S(2)}) async-start(bf16[8,4,32,1024]{3,2,1,0:T(8,128)(2,1)} %get-tuple-element.28), calls=%async_computation.6 | async-start | bytes 4194304 | tf_op jit(solution)/shard_map/all_to_all | solution.py:190
  755.8 4.3 copy-start.1
Sparse Core Ops, SparseCore 0:
  11.1 123.2 reduce-scatter.1
  191.5 85.4 all-gather.12
  278.9 227.5 all-gather.14
  508.2 87.4 all-gather.10
  597.4 87.4 all-gather.8
